TPU v7x, 32 devices: a whole 2x2x4 slice. The times are simulated.
32 devices in a mesh: heads: 8 (over z, y), model: 4 (over x, core).
Axes of the slice: x: 2, y: 2, z: 4, core: 2. Of those that a mesh axis runs over, the one named last changes fastest.
Arguments:
- hidden_in: bfloat16 [2048, 3840], P(None, 'model')
- seg_ids: int32 [2048], replicated
- positions: int32 [2048], replicated
- w_query: bfloat16 [2, 3840, 4096], P(None, 'model', 'heads')
- w_key: bfloat16 [2, 3840, 2048], P(None, 'model', 'heads')
- w_value: bfloat16 [2, 3840, 2048], P(None, 'model', 'heads')
- w_out: bfloat16 [2, 4096, 3840], P(None, 'heads', 'model')
- w_gate: bfloat16 [2, 3840, 15360], P(None, 'model', 'heads')
- w_up: bfloat16 [2, 3840, 15360], P(None, 'model', 'heads')
- w_down: bfloat16 [2, 15360, 3840], P(None, 'heads', 'model')
- norm_scales: float32 [2, 4, 3840], P(None, None, 'model')
- qk_scales: float32 [2, 2, 256], replicated
Outputs:
- output 1: bfloat16 [2048, 3840], P(None, 'model')
- output 2: bfloat16 [2, 2048, 8, 256], P(None, None, 'heads')
- output 3: bfloat16 [2, 2048, 8, 256], P(None, None, 'heads')
All inputs are finite; a program needn't handle non-finite values.
Results may differ from a plain program's by a relative error of at most 0.02.
Values are sent between devices in bfloat16 or wider.
A program may use at most 1 GiB of HBM per device.

v0:
```python
import jax
import jax.numpy as jnp
from jax import lax
from jax.sharding import PartitionSpec as P

NORM_EPS = 1e-6
Q_BLOCK = 256
WINDOW = 1024
GLOBAL_BASE = 1000000.0
GLOBAL_FACTOR = 8.0
LOCAL_BASE = 10000.0


def head_norm(values, scale_row):
    mean_sq = jnp.mean(values * values, axis=-1, keepdims=True)
    return values * lax.rsqrt(mean_sq + NORM_EPS) * (1.0 + scale_row)


def rope_tables(positions, head_dim, rope_base, pos_factor):
    exponents = jnp.arange(0, head_dim, 2).astype(jnp.float32) / head_dim
    inv_freq = rope_base ** (-exponents)
    angles = (positions.astype(jnp.float32) / pos_factor)[:, None] * inv_freq[None, :]
    return jnp.cos(angles), jnp.sin(angles)


def apply_rope(values, cos_tab, sin_tab):
    half_dim = values.shape[-1] // 2
    first_half = values[..., :half_dim]
    second_half = values[..., half_dim:]
    cos_bcast = cos_tab[:, None, :]
    sin_bcast = sin_tab[:, None, :]
    return jnp.concatenate([first_half * cos_bcast - second_half * sin_bcast, second_half * cos_bcast + first_half * sin_bcast], axis=-1)


def attend(query_heads, key_heads, value_heads, seg_ids, positions, window):
    n_tok, kv_count, head_dim = key_heads.shape
    group_size = query_heads.shape[1] // kv_count
    n_blocks = n_tok // Q_BLOCK
    q_scale = head_dim ** -0.5
    q_blocks = query_heads.reshape(n_blocks, Q_BLOCK, kv_count, group_size, head_dim)
    seg_blocks = seg_ids.reshape(n_blocks, Q_BLOCK)
    pos_blocks = positions.reshape(n_blocks, Q_BLOCK)

    def one_block(block_args):
        q_blk, seg_blk, pos_blk = block_args
        scores = jnp.einsum('qkgd,tkd->kgqt', q_blk, key_heads, preferred_element_type=jnp.float32) * q_scale
        pos_gap = pos_blk[:, None] - positions[None, :]
        allowed = (seg_blk[:, None] == seg_ids[None, :]) & (pos_gap >= 0) & (pos_gap < window)
        scores = jnp.where(allowed[None, None], scores, -1e30)
        row_max = jnp.max(scores, axis=-1, keepdims=True)
        exp_scores = jnp.exp(scores - row_max)
        probs_bf = (exp_scores / jnp.sum(exp_scores, axis=-1, keepdims=True)).astype(jnp.bfloat16)
        blk_out = jnp.einsum('kgqt,tkd->qkgd', probs_bf, value_heads, preferred_element_type=jnp.float32)
        return blk_out.astype(jnp.bfloat16)

    attn_out = lax.map(one_block, (q_blocks, seg_blocks, pos_blocks))
    return attn_out.reshape(n_tok, -1)


def solution(mesh):
    n_model = mesh.shape['model']
    col_spec = P(None, 'model', 'heads')
    row_spec = P(None, 'heads', 'model')
    cache_spec = P(None, None, 'heads', None)

    def body(hidden_in, seg_ids, positions, w_query, w_key, w_value, w_out, w_gate, w_up, w_down, norm_scales, qk_scales):
        n_tok = hidden_in.shape[0]
        head_dim = qk_scales.shape[-1]
        full_width = hidden_in.shape[1] * n_model

        def width_norm(values, scale_row):
            sq_sum = lax.psum(jnp.sum(values * values, axis=-1, keepdims=True), 'model')
            return values * lax.rsqrt(sq_sum / full_width + NORM_EPS) * (1.0 + scale_row)

        settings = ((GLOBAL_BASE, GLOBAL_FACTOR, n_tok), (LOCAL_BASE, 1.0, WINDOW))
        hidden = hidden_in
        key_list = []
        value_list = []
        for layer_idx in range(2):
            rope_base, pos_factor, window = settings[layer_idx]
            resid_f32 = hidden.astype(jnp.float32)
            normed = width_norm(resid_f32, norm_scales[layer_idx, 0]).astype(jnp.bfloat16)
            q_part, k_part, v_part = lax.psum((
                jnp.dot(normed, w_query[layer_idx], preferred_element_type=jnp.float32),
                jnp.dot(normed, w_key[layer_idx], preferred_element_type=jnp.float32),
                jnp.dot(normed, w_value[layer_idx], preferred_element_type=jnp.float32)), 'model')
            cos_tab, sin_tab = rope_tables(positions, head_dim, rope_base, pos_factor)
            query_heads = apply_rope(head_norm(q_part.astype(jnp.bfloat16).astype(jnp.float32).reshape(n_tok, -1, head_dim), qk_scales[layer_idx, 0]), cos_tab, sin_tab).astype(jnp.bfloat16)
            key_heads = apply_rope(head_norm(k_part.astype(jnp.bfloat16).astype(jnp.float32).reshape(n_tok, -1, head_dim), qk_scales[layer_idx, 1]), cos_tab, sin_tab).astype(jnp.bfloat16)
            value_heads = v_part.astype(jnp.bfloat16).reshape(n_tok, -1, head_dim)
            attn_out = attend(query_heads, key_heads, value_heads, seg_ids, positions, window)
            attn_sum = lax.psum(jnp.dot(attn_out, w_out[layer_idx], preferred_element_type=jnp.float32), 'heads').astype(jnp.bfloat16)
            hidden_mid = (resid_f32 + width_norm(attn_sum.astype(jnp.float32), norm_scales[layer_idx, 1])).astype(jnp.bfloat16)
            mid_f32 = hidden_mid.astype(jnp.float32)
            normed_ffn = width_norm(mid_f32, norm_scales[layer_idx, 2]).astype(jnp.bfloat16)
            gate_part, up_part = lax.psum((
                jnp.dot(normed_ffn, w_gate[layer_idx], preferred_element_type=jnp.float32),
                jnp.dot(normed_ffn, w_up[layer_idx], preferred_element_type=jnp.float32)), 'model')
            gate_act = jax.nn.gelu(gate_part.astype(jnp.bfloat16).astype(jnp.float32), approximate=True)
            ffn_in = (gate_act * up_part.astype(jnp.bfloat16).astype(jnp.float32)).astype(jnp.bfloat16)
            ffn_sum = lax.psum(jnp.dot(ffn_in, w_down[layer_idx], preferred_element_type=jnp.float32), 'heads').astype(jnp.bfloat16)
            hidden = (mid_f32 + width_norm(ffn_sum.astype(jnp.float32), norm_scales[layer_idx, 3])).astype(jnp.bfloat16)
            key_list.append(key_heads)
            value_list.append(value_heads)
        return hidden, jnp.stack(key_list), jnp.stack(value_list)

    return jax.shard_map(body, mesh=mesh,
                         in_specs=(P(None, 'model'), P(), P(), col_spec, col_spec, col_spec, row_spec, col_spec, col_spec, row_spec, P(None, None, 'model'), P()),
                         out_specs=(P(None, 'model'), cache_spec, cache_spec),
                         check_vma=False)
```

profile of v0, /device:TPU:0, one launch (start us, length us, event | category | flops | bytes accessed | tf_op | source)
XLA Modules:
  0.0 2945.9 jit_solution(1733640165379392938)
XLA Ops:
  5.1 8.6 psum.154
  13.7 7.0 fusion.130
  26.9 147.1 %all-reduce.12 = (bf16[2048,512]{1,0:T(8,128)(2,1)S(1)}, bf16[2048,256]{1,0:T(8,128)(2,1)}, bf16[2048,256]{1,0:T(8,128)(2,1)}) all-reduce(f32[2048,512]{1,0:T(8,128)} %fusion.130, f32[2048,256]{1,0:T(8,128)} %fusion.142, f32[2048,256]{1,0:T(8,128)} %fusion.140), channel_id=1, replica_groups=mesh['heads'=8,'model'=4] {'model'}, use_global_device_ids=true, to_apply=%region_2.0 | all-reduce | flops 2097152 | bytes 12582912 | tf_op jit(solution)/shard_map/psum | solution.py:83
  198.0 36.4 %while.20 = (s32[]{:T(128)}, bf16[8,256,1,2,256]{4,1,3,2,0:T(8,128)(2,1)S(1)}, s32[8,256]{1,0:T(8,128)S(1)}, s32[2048]{0:T(1024)S(1)}, s32[8,256]{1,0:T(8,128)S(...) while((s32[]{:T(128)}, ...), condition=%wide.region_10.11_spmd, body=%wide.region_7.10_spmd.sunk | while | flops 1085406208 | bytes 20480648 | solution.py:56
  245.2 304.6 %all-reduce.13 = bf16[2048,960]{0,1:T(8,128)(2,1)} all-reduce(f32[2048,960]{0,1:T(8,128)} %fusion.128), channel_id=1, replica_groups=mesh['heads'=8,'model'=4] {'heads'}, use_global_device_ids=true, to_apply=%region_11.12 | all-reduce | flops 1966080 | bytes 11796480 | tf_op jit(solution)/shard_map/psum | solution.py:92
  570.4 15.6 fusion.90
  586.0 14.6 fusion.88
  600.6 535.0 %all-reduce.14 = (bf16[2048,1920]{1,0:T(8,128)(2,1)}, bf16[2048,1920]{1,0:T(8,128)(2,1)}) all-reduce(f32[2048,1920]{1,0:T(8,128)} %fusion.88, f32[2048,1920]{1,0:T(8,128)} %fusion.90), channel_id=1, replica_groups=mesh['heads'=8,'model'=4] {'model'}, use_global_device_ids=true, to_apply=%region_17.18 | all-reduce | flops 7864320 | bytes 47185920 | tf_op jit(solution)/shard_map/psum | solution.py:96
  1135.6 15.1 fusion.78
  1150.7 306.4 %all-reduce.15 = bf16[2048,960]{0,1:T(8,128)(2,1)} all-reduce(f32[2048,960]{0,1:T(8,128)} %fusion.78), channel_id=1, replica_groups=mesh['heads'=8,'model'=4] {'heads'}, use_global_device_ids=true, to_apply=%region_18.19 | all-reduce | flops 1966080 | bytes 11796480 | tf_op jit(solution)/shard_map/psum | solution.py:101
  1465.9 6.1 fusion.68
  1472.0 6.2 psum.165
  1491.1 146.2 %all-reduce.16 = (bf16[2048,512]{1,0:T(8,128)(2,1)S(1)}, bf16[2048,256]{1,0:T(8,128)(2,1)S(1)}, bf16[2048,256]{1,0:T(8,128)(2,1)}) all-reduce(f32[2048,512]{1,0:T(8,128)} %fusion.126, f32[2048,256]{1,0:T(8,128)} %fusion.138, f32[2048,256]{1,0:T(8,128)} %fusion.136), channel_id=1, replica_groups=mesh['heads'=8,'model'=4] {'model'}, use_global_device_ids=true, to_apply=%region_23.24 | all-reduce | flops 2097152 | bytes 12582912 | tf_op jit(solution)/shard_map/psum | solution.py:83
  1663.2 36.4 %while.21 = (s32[]{:T(128)}, bf16[8,256,1,2,256]{4,1,3,2,0:T(8,128)(2,1)S(1)}, s32[8,256]{1,0:T(8,128)S(1)}, s32[2048]{0:T(1024)S(1)}, s32[8,256]{1,0:T(8,128)S(...) while((s32[]{:T(128)}, ...), condition=%wide.region_31.32_spmd, body=%wide.region_28.31_spmd.sunk | while | flops 1085406208 | bytes 20480648 | solution.py:56
  1710.4 305.5 %all-reduce.17 = bf16[2048,960]{0,1:T(8,128)(2,1)} all-reduce(f32[2048,960]{0,1:T(8,128)} %fusion.124), channel_id=1, replica_groups=mesh['heads'=8,'model'=4] {'heads'}, use_global_device_ids=true, to_apply=%region_32.33 | all-reduce | flops 1966080 | bytes 11796480 | tf_op jit(solution)/shard_map/psum | solution.py:92
  2018.8 8.6 psum.170
  2033.4 6.9 psum.171
  2040.3 15.8 fusion.85
  2056.2 14.6 fusion.83
  2070.8 534.0 %all-reduce.18 = (bf16[2048,1920]{1,0:T(8,128)(2,1)}, bf16[2048,1920]{1,0:T(8,128)(2,1)}) all-reduce(f32[2048,1920]{1,0:T(8,128)} %fusion.83, f32[2048,1920]{1,0:T(8,128)} %fusion.85), channel_id=1, replica_groups=mesh['heads'=8,'model'=4] {'model'}, use_global_device_ids=true, to_apply=%region_38.39 | all-reduce | flops 7864320 | bytes 47185920 | tf_op jit(solution)/shard_map/psum | solution.py:96
  2604.7 15.1 fusion.76
  2619.8 304.1 %all-reduce.19 = bf16[2048,960]{0,1:T(8,128)(2,1)} all-reduce(f32[2048,960]{0,1:T(8,128)} %fusion.76), channel_id=1, replica_groups=mesh['heads'=8,'model'=4] {'heads'}, use_global_device_ids=true, to_apply=%region_39.40 | all-reduce | flops 1966080 | bytes 11796480 | tf_op jit(solution)/shard_map/psum | solution.py:101
  2926.9 11.1 psum.175
  2938.0 7.7 fusion.75
  (238 shorter events, 207.5 us)
Async XLA Ops:
  13.7 7.0 copy-start
  13.7 7.0 copy-start.27
  20.7 3.1 copy-start.29
  191.7 6.1 copy-start.15
  199.0 2.8 copy-start.11
  203.5 2.8 copy-start.11
  217.1 2.8 copy-start.11
  570.4 15.6 copy-start.3
  1150.7 315.2 %copy-start.18 = (f32[1,1,960]{2,1,0:T(1,128)S(1)}, f32[1,1,960]{2,1,0:T(1,128)}, u32[]{:S(2)}) copy-start(f32[1,1,960]{2,1,0:T(1,128)} %get-tuple-element.224) | copy-start | bytes 11524
  1465.9 12.4 copy-start.22
  1465.9 12.4 copy-start.28
  1478.3 5.2 copy-start.2
  1478.3 5.2 copy-start.30
  1483.5 3.1 copy-start.24
  1491.1 146.6 %copy-start.20 = (f32[1,1,256]{2,1,0:T(1,128)S(1)}, f32[1,1,256]{2,1,0:T(1,128)}, u32[]{:S(2)}) copy-start(f32[1,1,256]{2,1,0:T(1,128)} %get-tuple-element.233) | copy-start | bytes 3076
  1637.4 5.5 copy-start.5
  1637.4 5.5 copy-start.7
  1637.4 5.5 copy-start.12
  1637.4 5.5 copy-start.13
  1664.2 2.8 copy-start.14
  1710.4 317.0 %copy-start.17 = (f32[1,1,960]{2,1,0:T(1,128)S(1)}, f32[1,1,960]{2,1,0:T(1,128)}, u32[]{:S(2)}) copy-start(f32[1,1,960]{2,1,0:T(1,128)} %get-tuple-element.222) | copy-start | bytes 11524
  2027.4 12.9 copy-start.21
  2040.3 15.9 copy-start.1
  2619.8 318.2 %copy-start.16 = (f32[1,1,960]{2,1,0:T(1,128)S(1)}, f32[1,1,960]{2,1,0:T(1,128)}, u32[]{:S(2)}) copy-start(f32[1,1,960]{2,1,0:T(1,128)} %get-tuple-element.228) | copy-start | bytes 11524
  (21 other events, 46.9 us)
where the time goes:
time: 2950 us
  blocking collectives  2640 us (89%)
  matrix products  175 us (6%)
  other arithmetic  105 us (4%)
    psum x2, blocking collectives, body(): lax.psum((jnp.dot(normed_ffn, w_gate[layer_idx], preferred_element_type=j...  1070 us
    psum x2, blocking collectives, body(): lax.psum(jnp.dot(ffn_in, w_down[layer_idx], preferred_element_type=jnp.fl...  610 us
    psum x2, blocking collectives, body(): lax.psum(jnp.dot(attn_out, w_out[layer_idx], preferred_element_type=jnp.f...  610 us
    psum x2, blocking collectives, body(): lax.psum((jnp.dot(normed, w_query[layer_idx], preferred_element_type=jnp....  293 us

commit v1 on v0

v1 whole, which is shorter than its diff:
```python
import functools

import jax
import jax.numpy as jnp
from jax import lax
from jax.experimental import pallas as pl
from jax.experimental.pallas import tpu as pltpu
from jax.sharding import PartitionSpec as P

NORM_EPS = 1e-6
WINDOW = 1024
GLOBAL_BASE = 1000000.0
GLOBAL_FACTOR = 8.0
LOCAL_BASE = 10000.0
MESH = pl.DeviceIdType.MESH
N_ROWS = 64
PIECES = 8
HALF = 32


def remote(src, dst, send_sem, recv_sem, device):
    return pltpu.make_async_remote_copy(src_ref=src, dst_ref=dst, send_sem=send_sem, recv_sem=recv_sem,
                                        device_id=device, device_id_type=MESH)


def move_kernel(mode, *refs):
    if mode == 'first':
        (hid_ref, scale_b_ref, x_out, g_out,
         loc_sem, a2a_s, a2a_r, gr_s, gr_r, gl_s, gl_r, gy_s, gy_r) = refs
    elif mode == 'mid':
        (part_ref, x_ref, scale_a_ref, scale_b_ref, x_out, g_out,
         sums, y_buf, r_buf, l_buf, loc_sem, y_s, y_r, r_s, r_r, l_s, l_r,
         gr_s, gr_r, gl_s, gl_r, gy_s, gy_r) = refs
    else:
        (part_ref, x_ref, scale_a_ref, g_out,
         sums, y_buf, r_buf, l_buf, fin, loc_sem, y_s, y_r, r_s, r_r, l_s, l_r,
         a2a_s, a2a_r, gr_s, gr_r, gl_s, gl_r, gy_s, gy_r) = refs
    head = lax.axis_index('heads')
    m = lax.axis_index('model')
    z = lax.div(head, 2)
    y = lax.rem(head, 2)
    x = lax.div(m, 2)
    c = lax.rem(m, 2)
    flips = [None, x * 2 + (1 - c), (1 - x) * 2 + c, (1 - x) * 2 + (1 - c)]
    y_peer = (z * 2 + 1 - y, m)
    up = (z * 2 + 2 + y, m)
    down = (z * 2 - 2 + y, m)

    barrier = pltpu.get_barrier_semaphore()

    def greet(device):
        pl.semaphore_signal(barrier, inc=1, device_id=device, device_id_type=MESH)

    greet(y_peer)
    pl.when(z < 3)(lambda: greet(up))
    pl.when(z > 0)(lambda: greet(down))
    n_wait = 2
    if mode != 'mid':
        for j in (1, 2, 3):
            greet((head, flips[j]))
        n_wait = 5
    inside = lax.rem(lax.div(z + 1, 2), 2)
    pl.semaphore_wait(barrier, n_wait + inside)

    if mode == 'first':
        own = pltpu.make_async_copy(hid_ref.at[m, head], x_out.at[0], loc_sem.at[0])
        own.start()
        sends = [remote(hid_ref.at[flips[j], head], x_out.at[j], a2a_s.at[j], a2a_r.at[j], (head, flips[j]))
                 for j in (1, 2, 3)]
        for copy in sends:
            copy.start()
        own.wait()
        for copy in sends:
            copy.wait()
    else:
        def at_piece(p):
            return lax.div(p, 2), pl.ds(pl.multiple_of(lax.rem(p, 2) * HALF, HALF), HALF)

        def load_of(p):
            j, rows = at_piece(p)
            return pltpu.make_async_copy(part_ref.at[j, :, y, rows, :], sums.at[j, :, rows, :], loc_sem.at[p])

        def y_of(p):
            j, rows = at_piece(p)
            return remote(part_ref.at[j, :, 1 - y, rows, :], y_buf.at[j, :, rows, :], y_s.at[p], y_r.at[p], y_peer)

        def r_of(t, p):
            j, rows = at_piece(p)
            return remote(sums.at[j, t, rows, :], r_buf.at[t - 1, j, rows, :], r_s.at[t - 1, p], r_r.at[t - 1, p], up)

        def l_of(t, p):
            j, rows = at_piece(p)
            return remote(sums.at[j, t, rows, :], l_buf.at[t, j, rows, :], l_s.at[t, p], l_r.at[t, p], down)

        for p in range(PIECES):
            y_of(p).start()
            load_of(p).start()

        def step(s, carry):
            @pl.when(s < PIECES)
            def _():
                load_of(s).wait()
                y_of(s).wait_recv()
                j, rows = at_piece(s)
                sums[j, :, rows, :] += y_buf[j, :, rows, :]

            p_r = s - z

            @pl.when((p_r >= 0) & (p_r < PIECES))
            def _():
                j, rows = at_piece(p_r)
                for t in (3, 2, 1):
                    @pl.when((z > 0) & (z <= t))
                    def _():
                        r_of(t, p_r).wait_recv()
                        sums[j, t, rows, :] += r_buf[t - 1, j, rows, :]

                    @pl.when(z < t)
                    def _():
                        r_of(t, p_r).start()

            p_l = s - (3 - z)

            @pl.when((p_l >= 0) & (p_l < PIECES))
            def _():
                j, rows = at_piece(p_l)
                for t in (0, 1, 2):
                    @pl.when((z < 3) & (z >= t))
                    def _():
                        l_of(t, p_l).wait_recv()
                        sums[j, t, rows, :] += l_buf[t, j, rows, :]

                    @pl.when(z > t)
                    def _():
                        l_of(t, p_l).start()
            return carry

        lax.fori_loop(0, PIECES + 3, step, 0)

    width = 4 * 960

    def inv_rms(parts):
        total = functools.reduce(lambda a, b: a + b, [jnp.sum(v * v, axis=-1, keepdims=True) for v in parts])
        return lax.rsqrt(total / width + NORM_EPS)

    if mode == 'first':
        rows_new = [x_out[j].astype(jnp.float32) for j in range(4)]
    else:
        added = [sums[j, z].astype(jnp.bfloat16).astype(jnp.float32) for j in range(4)]
        inv = inv_rms(added)
        rows_new = []
        for j in range(4):
            new = (x_ref[j].astype(jnp.float32) + added[j] * inv * (1.0 + scale_a_ref[j])).astype(jnp.bfloat16)
            if mode == 'mid':
                x_out[j] = new
                rows_new.append(new.astype(jnp.float32))
            else:
                fin[j] = new
    if mode != 'last':
        inv = inv_rms(rows_new)
        for j in range(4):
            g_out[j, head] = (rows_new[j] * inv * (1.0 + scale_b_ref[j])).astype(jnp.bfloat16)
    else:
        own = pltpu.make_async_copy(fin.at[0], g_out.at[m, head], loc_sem.at[PIECES])
        own.start()
        sends = [remote(fin.at[j], g_out.at[m, head], a2a_s.at[j], a2a_r.at[j], (head, flips[j])) for j in (1, 2, 3)]
        for copy in sends:
            copy.start()
        own.wait()
        for j, copy in zip((1, 2, 3), sends):
            copy.wait_send()
            remote(fin.at[j], g_out.at[flips[j], head], a2a_s.at[j], a2a_r.at[j], (head, flips[j])).wait_recv()

    def gather(kind, bz):
        send_sems, recv_sems, device = {'r': (gr_s, gr_r, up), 'l': (gl_s, gl_r, down), 'y': (gy_s, gy_r, y_peer)}[kind]
        block = g_out.at[:, bz * 2 + y]
        return remote(block, block, send_sems.at[bz], recv_sems.at[bz], device)

    gather('y', z).start()
    pl.when(z < 3)(lambda: gather('r', z).start())
    pl.when(z > 0)(lambda: gather('l', z).start())
    for d in (1, 2, 3):
        @pl.when(z >= d)
        def _():
            gather('r', z - d).wait_recv()
            pl.when(z < 3)(lambda: gather('r', z - d).start())
            gather('y', z - d).start()

        @pl.when(z + d <= 3)
        def _():
            gather('l', z + d).wait_recv()
            pl.when(z > 0)(lambda: gather('l', z + d).start())
            gather('y', z + d).start()
    for bz in range(4):
        gather('y', bz).wait_send()
        block = g_out.at[:, bz * 2 + 1 - y]
        remote(block, block, gy_s.at[bz], gy_r.at[bz], y_peer).wait_recv()
        pl.when((bz <= z) & (z < 3))(lambda: gather('r', bz).wait_send())
        pl.when((bz >= z) & (z > 0))(lambda: gather('l', bz).wait_send())

    if mode != 'first':
        def drain(p, carry):
            y_of(p).wait_send()
            for t in (1, 2, 3):
                pl.when(z < t)(lambda: r_of(t, p).wait_send())
            for t in (0, 1, 2):
                pl.when(z > t)(lambda: l_of(t, p).wait_send())
            return carry

        lax.fori_loop(0, PIECES, drain, 0)


def move(mode, call_id, *args):
    vmem = pl.BlockSpec(memory_space=pltpu.VMEM)
    hbm = pl.BlockSpec(memory_space=pl.ANY)
    dma = pltpu.SemaphoreType.DMA
    rows_shape = jax.ShapeDtypeStruct((4, N_ROWS, 960), jnp.bfloat16)
    g_shape = jax.ShapeDtypeStruct((4, 8, N_ROWS, 960), jnp.bfloat16)
    ring = [dma((4,))] * 6
    a2a = [dma((4,)), dma((4,))]
    reduce_bufs = [pltpu.VMEM((4, 4, N_ROWS, 960), jnp.float32), pltpu.VMEM((4, 4, N_ROWS, 960), jnp.float32),
                   pltpu.VMEM((3, 4, N_ROWS, 960), jnp.float32), pltpu.VMEM((3, 4, N_ROWS, 960), jnp.float32)]
    reduce_sems = [dma((PIECES + 1,)), dma((PIECES,)), dma((PIECES,))] + [dma((3, PIECES))] * 4
    if mode == 'first':
        in_specs, outs = [hbm, vmem], (rows_shape, g_shape)
        scratch = [dma((1,))] + a2a + ring
    elif mode == 'mid':
        in_specs, outs = [hbm, vmem, vmem, vmem], (rows_shape, g_shape)
        scratch = reduce_bufs + reduce_sems + ring
    else:
        in_specs, outs = [hbm, vmem, vmem], (g_shape,)
        scratch = reduce_bufs + [pltpu.VMEM((4, N_ROWS, 960), jnp.bfloat16)] + reduce_sems + a2a + ring
    micros = {'first': 55, 'mid': 140, 'last': 150}[mode]
    return pl.pallas_call(
        functools.partial(move_kernel, mode),
        out_shape=outs,
        in_specs=in_specs,
        out_specs=tuple(vmem for _ in outs),
        scratch_shapes=scratch,
        name='move_' + mode + str(call_id),
        cost_estimate=pl.CostEstimate(flops=micros * 15_000_000, bytes_accessed=1 << 24, transcendentals=0),
        compiler_params=pltpu.CompilerParams(collective_id=call_id, has_side_effects=True, vmem_limit_bytes=50 << 20),
    )(*args)


def kv_kernel(kv_ref, out_ref, loc_sem, send_sems, recv_sems):
    head = lax.axis_index('heads')
    m = lax.axis_index('model')
    x = lax.div(m, 2)
    c = lax.rem(m, 2)
    m_core, m_x, m_both = x * 2 + 1 - c, (1 - x) * 2 + c, (1 - x) * 2 + 1 - c
    barrier = pltpu.get_barrier_semaphore()
    for peer in (m_core, m_x):
        pl.semaphore_signal(barrier, inc=1, device_id=(head, peer), device_id_type=MESH)
    pl.semaphore_wait(barrier, 2)
    own = pltpu.make_async_copy(kv_ref, out_ref.at[m], loc_sem.at[0])

    def send(slot, src, place, peer):
        return remote(src, out_ref.at[place], send_sems.at[slot], recv_sems.at[slot], (head, peer))

    to_x = send(0, kv_ref, m, m_x)
    to_core = send(1, kv_ref, m, m_core)
    to_x.start()
    to_core.start()
    own.start()
    send(0, kv_ref, m_x, m_x).wait_recv()
    on = send(2, out_ref.at[m_x], m_x, m_core)
    on.start()
    own.wait()
    send(1, kv_ref, m_core, m_core).wait_recv()
    send(2, kv_ref, m_both, m_core).wait_recv()
    to_x.wait_send()
    to_core.wait_send()
    on.wait_send()


def share_kv(call_id, kv):
    vmem = pl.BlockSpec(memory_space=pltpu.VMEM)
    dma = pltpu.SemaphoreType.DMA
    return pl.pallas_call(
        kv_kernel,
        out_shape=jax.ShapeDtypeStruct((4,) + kv.shape, kv.dtype),
        in_specs=[vmem], out_specs=vmem,
        scratch_shapes=[dma((1,)), dma((3,)), dma((3,))],
        name='share_kv' + str(call_id),
        cost_estimate=pl.CostEstimate(flops=20 * 15_000_000, bytes_accessed=1 << 22, transcendentals=0),
        compiler_params=pltpu.CompilerParams(collective_id=call_id, has_side_effects=True),
    )(kv)


def head_norm(values, scale_row):
    mean_sq = jnp.mean(values * values, axis=-1, keepdims=True)
    return values * lax.rsqrt(mean_sq + NORM_EPS) * (1.0 + scale_row)


def rope_tables(positions, head_dim, rope_base, pos_factor):
    exponents = jnp.arange(0, head_dim, 2).astype(jnp.float32) / head_dim
    inv_freq = rope_base ** (-exponents)
    angles = (positions.astype(jnp.float32) / pos_factor)[:, None] * inv_freq[None, :]
    return jnp.cos(angles), jnp.sin(angles)


def apply_rope(values, cos_tab, sin_tab):
    half_dim = values.shape[-1] // 2
    first_half = values[..., :half_dim]
    second_half = values[..., half_dim:]
    cos_bcast = cos_tab[:, None, :]
    sin_bcast = sin_tab[:, None, :]
    return jnp.concatenate([first_half * cos_bcast - second_half * sin_bcast, second_half * cos_bcast + first_half * sin_bcast], axis=-1)


def attend(q, keys, values, seg_q, pos_q, seg_ids, positions, window):
    scores = jnp.einsum('qgd,td->gqt', q, keys, preferred_element_type=jnp.float32) * (q.shape[-1] ** -0.5)
    gap = pos_q[:, None] - positions[None, :]
    allowed = (seg_q[:, None] == seg_ids[None, :]) & (gap >= 0) & (gap < window)
    scores = jnp.where(allowed[None], scores, -1e30)
    exp_scores = jnp.exp(scores - jnp.max(scores, axis=-1, keepdims=True))
    probs = (exp_scores / jnp.sum(exp_scores, axis=-1, keepdims=True)).astype(jnp.bfloat16)
    out = jnp.einsum('gqt,td->qgd', probs, values, preferred_element_type=jnp.float32)
    return out.astype(jnp.bfloat16).reshape(q.shape[0], -1)


def solution(mesh):
    col_spec = P(None, 'model', 'heads')
    row_spec = P(None, 'heads', 'model')
    cache_spec = P(None, None, 'heads', None)
    over_core = [(0, 1), (1, 0), (2, 3), (3, 2)]
    over_x = [(0, 2), (2, 0), (1, 3), (3, 1)]

    def spread(w):
        by_x = lax.ppermute(w, 'model', over_x)
        return [w, lax.ppermute(w, 'model', over_core), by_x, lax.ppermute(by_x, 'model', over_core)]

    def body(hidden_in, seg_ids, positions, w_query, w_key, w_value, w_out, w_gate, w_up, w_down, norm_scales, qk_scales):
        n_tok = hidden_in.shape[0]
        head_dim = qk_scales.shape[-1]
        m = lax.axis_index('model')
        n_own = n_tok // 4
        scales = jnp.stack(spread(norm_scales))[:, :, :, None, :]
        seg_q = lax.dynamic_slice_in_dim(seg_ids, m * n_own, n_own)
        pos_q = lax.dynamic_slice_in_dim(positions, m * n_own, n_own)

        def dot(a, b):
            return jnp.dot(a, b, preferred_element_type=jnp.float32)

        def summed(g, ws):
            acc = dot(g[0], ws[0])
            for j in (1, 2, 3):
                acc = acc + dot(g[j], ws[j])
            return acc.astype(jnp.bfloat16)

        def chunks(a, ws):
            return jnp.stack([dot(a, w) for w in ws]).reshape(4, 4, 2, N_ROWS, 960)

        rows, gathered = move('first', 0, hidden_in.reshape(4, 8, N_ROWS, 960), scales[:, 0, 0])
        settings = ((GLOBAL_BASE, GLOBAL_FACTOR, n_tok), (LOCAL_BASE, 1.0, WINDOW))
        key_list, value_list = [], []
        for l in range(2):
            rope_base, pos_factor, window = settings[l]
            wq, wk, wv, wo, wg, wu, wd = [spread(w[l]) for w in (w_query, w_key, w_value, w_out, w_gate, w_up, w_down)]
            g = gathered.reshape(4, n_own, 960)
            cos_tab, sin_tab = rope_tables(pos_q, head_dim, rope_base, pos_factor)

            def heads_of(ws, row):
                vals = summed(g, ws).astype(jnp.float32).reshape(n_own, -1, head_dim)
                return apply_rope(head_norm(vals, qk_scales[l, row]), cos_tab, sin_tab).astype(jnp.bfloat16)

            q = heads_of(wq, 0)
            k = heads_of(wk, 1)
            v = summed(g, wv)
            kv = share_kv(1 + 4 * l, jnp.stack([k.reshape(n_own, head_dim), v]))
            keys = kv[:, 0].reshape(n_tok, head_dim)
            values = kv[:, 1].reshape(n_tok, head_dim)
            key_list.append(keys)
            value_list.append(values)
            o = attend(q, keys, values, seg_q, pos_q, seg_ids, positions, window)
            rows, gathered = move('mid', 2 + 4 * l, chunks(o, wo), rows, scales[:, l, 1], scales[:, l, 2])
            g = gathered.reshape(4, n_own, 960)
            gate = jax.nn.gelu(summed(g, wg).astype(jnp.float32), approximate=True)
            mid = (gate * summed(g, wu).astype(jnp.float32)).astype(jnp.bfloat16)
            part = chunks(mid, wd)
            if l == 0:
                rows, gathered = move('mid', 3 + 4 * l, part, rows, scales[:, l, 3], scales[:, 1, 0])
            else:
                hidden, = move('last', 3 + 4 * l, part, rows, scales[:, l, 3])
        return hidden.reshape(n_tok, 960), jnp.stack(key_list)[:, :, None], jnp.stack(value_list)[:, :, None]

    return jax.shard_map(body, mesh=mesh,
                         in_specs=(P(None, 'model'), P(), P(), col_spec, col_spec, col_spec, row_spec, col_spec, col_spec, row_spec, P(None, None, 'model'), P()),
                         out_specs=(P(None, 'model'), cache_spec, cache_spec),
                         check_vma=False)
```

time: 2950 us -> 1280 us (0.43)
  blocking collectives: 2640 us -> 0 us
  Pallas kernels: 0 us -> 909 us
  other arithmetic: 105 us -> 37.7 us
  waiting for transfers between devices: 0 us -> 51.6 us
  local copies, waits for them, and re-layouts: 21.2 us -> 63.9 us
    psum x16 -> x0, blocking collectives: 2640 us -> none  [the longest x2 1070 us: body(): lax.psum((jnp.dot(normed_ffn, w_gate[layer_idx], preferred_element_type=j...]
    pallas_call x0 -> x7, Pallas kernels: none -> 909 us  [the longest x5 712 us: move(): pl.pallas_call(functools.partial(move_kernel, mode), out_shape=outs, in_s...]
    reduce_sum x28 -> x0, other arithmetic: 55.4 us -> none  [the longest x8 32.8 us: width_norm(): sq_sum = lax.psum(jnp.sum(values * values, axis=-1, keepdims=True), 'model')]
    ppermute x0 -> x45, waiting for transfers between devices: none -> 51.6 us  [the longest x15 46.5 us: spread(): by_x = lax.ppermute(w, 'model', over_x)]
    dot_general x46 -> x58, matrix products: 175 us -> 169 us  [the longest x56 159 us: dot(): return jnp.dot(a, b, preferred_element_type=jnp.float32)]
  transfers between devices with their start and end apart: 0 -> 45, of which waited for: 0 -> 6; matrix products, arithmetic and copies ran while one was open for 0% -> 21% of each run, Pallas kernels for 0% -> 58%
where the time goes in v1:
time: 1280 us; the launch traced here: 1270 us
  Pallas kernels  909 us (71%)
  matrix products  180 us (14%)
  local copies, waits for them, and re-layouts  63.9 us (5%)
  waiting for transfers between devices  51.6 us (4%)
  other arithmetic  37.7 us (3%)
  starting transfers between devices  25.7 us (2%)
    pallas_call x5, Pallas kernels, move(): pl.pallas_call(functools.partial(move_kernel, mode), out_shape=outs, in_s...  712 us
    pallas_call x2, Pallas kernels, share_kv(): pl.pallas_call(kv_kernel, out_shape=jax.ShapeDtypeStruct((4,) + kv.shape,...  197 us
    dot_general x56, matrix products, dot(): return jnp.dot(a, b, preferred_element_type=jnp.float32)  159 us
    ppermute x15, waiting for transfers between devices, spread(): by_x = lax.ppermute(w, 'model', over_x)  46.5 us
  transfers between devices with their start and end apart: 45, of which 6 were waited for; matrix products, arithmetic and copies ran while one was open for 21% of the time, Pallas kernels for 58%

profile of v1, /device:TPU:0, one launch (start us, length us, event | category | flops | bytes accessed | tf_op | source)
XLA Modules:
  0.0 1270.0 jit_solution(15134367275331051742)
XLA Ops:
  12.8 7.7 fusion.10
  30.2 6.7 slice_bitcast_fusion.4
  40.9 6.4 copy.48
  49.3 72.5 %move_first0.1 = (bf16[4,64,960]{2,1,0:T(8,128)(2,1)S(1)}, bf16[4,8,64,960]{3,2,1,0:T(8,128)(2,1)}) custom-call(bf16[4,8,64,960]{3,2,1,0:T(8,128)(2,1)} %bitcast.336, f32[4,1,960]{2,1,0:T(1,128)S(1)} %get-tuple-element.76.refs_1_), custom_call_target="tpu_custom_call" | custom-call | flops 825000000 | bytes 16777216 | tf_op jit(solution)/shard_map/move_first0/pallas_call | solution.py:234
  138.0 14.2 %collective-permute-done.10 = bf16[960,512]{1,0:T(8,128)(2,1)} collective-permute-done((bf16[960,512]{1,0:T(8,128)(2,1)}, bf16[960,512]{1,0:T(8,128)(2,1)}, u32[]{:S(2)}, u32[]{:S(2)}) %collective-permute-start.10) | collective-permute-done | bytes 983072 | tf_op jit(solution)/shard_map/ppermute | solution.py:331
  155.0 29.8 %share_kv1.1 = bf16[4,2,512,256]{3,2,1,0:T(8,128)(2,1)} custom-call(bf16[2,512,256]{2,1,0:T(8,128)(2,1)} %pad_maximum_fusion.4.kv_ref), custom_call_target="tpu_custom_call" | custom-call | flops 300000000 | bytes 4194304 | tf_op jit(solution)/shard_map/share_kv1/pallas_call | solution.py:280
  225.9 156.1 %move_mid2.1 = (bf16[4,64,960]{2,1,0:T(8,128)(2,1)S(1)}, bf16[4,8,64,960]{3,2,1,0:T(8,128)(2,1)}) custom-call(f32[4,4,2,64,960]{4,3,2,1,0:T(8,128)} %pad_maximum_fusion.refs_0_, bf16[4,64,960]{2,1,0:T(8,128)(2,1)S(1)} %get-tuple-element.12.refs_1_, f32[4,1,960]{2,1,0:T(1,128)S(1)} %get-tuple-element.75.refs_2_, f32[4,1,960]{2,1,0:T(1,128)S(1)} %get-tuple-element.74.refs_3_), custom_call_target="tpu_custom_call" | custom-call | flops 2100000000 | bytes 16777216 | tf_op jit(solution)/shard_map/move_mid2/pallas_call | solution.py:234
  398.5 6.3 fusion.124
  411.5 16.4 %collective-permute-done.22 = bf16[1920,960]{0,1:T(8,128)(2,1)} collective-permute-done((bf16[1920,960]{0,1:T(8,128)(2,1)}, bf16[1920,960]{0,1:T(8,128)(2,1)}, u32[]{:S(2)}, u32[]{:S(2)}) %collective-permute-start.22) | collective-permute-done | bytes 3686432 | tf_op jit(solution)/shard_map/ppermute | solution.py:331
  427.9 6.3 fusion.123
  442.4 9.2 fusion.21
  460.9 8.1 collective-permute-done.31
  475.7 156.7 %move_mid3.1 = (bf16[4,64,960]{2,1,0:T(8,128)(2,1)S(1)}, bf16[4,8,64,960]{3,2,1,0:T(8,128)(2,1)}) custom-call(f32[4,4,2,64,960]{4,3,2,1,0:T(8,128)} %pad_maximum_fusion.1.refs_0_, bf16[4,64,960]{2,1,0:T(8,128)(2,1)S(1)} %get-tuple-element.14.refs_1_, f32[4,1,960]{2,1,0:T(1,128)S(1)} %get-tuple-element.73.refs_2_, f32[4,1,960]{2,1,0:T(1,128)S(1)} %get-tuple-element.72.refs_3_), custom_call_target="tpu_custom_call" | custom-call | flops 2100000000 | bytes 16777216 | tf_op jit(solution)/shard_map/move_mid3/pallas_call | solution.py:234
  643.0 7.8 collective-permute-done.28
  673.7 167.4 %share_kv5.1 = bf16[4,2,512,256]{3,2,1,0:T(8,128)(2,1)} custom-call(bf16[2,512,256]{2,1,0:T(8,128)(2,1)} %pad_maximum_fusion.6.kv_ref), custom_call_target="tpu_custom_call" | custom-call | flops 300000000 | bytes 4194304 | tf_op jit(solution)/shard_map/share_kv5/pallas_call | solution.py:280
  869.9 157.7 %move_mid6.1 = (bf16[4,64,960]{2,1,0:T(8,128)(2,1)S(1)}, bf16[4,8,64,960]{3,2,1,0:T(8,128)(2,1)}) custom-call(f32[4,4,2,64,960]{4,3,2,1,0:T(8,128)} %pad_maximum_fusion.2.refs_0_, bf16[4,64,960]{2,1,0:T(8,128)(2,1)S(1)} %get-tuple-element.16.refs_1_, f32[4,1,960]{2,1,0:T(1,128)S(1)} %get-tuple-element.71.refs_2_, f32[4,1,960]{2,1,0:T(1,128)S(1)} %get-tuple-element.70.refs_3_), custom_call_target="tpu_custom_call" | custom-call | flops 2100000000 | bytes 16777216 | tf_op jit(solution)/shard_map/move_mid6/pallas_call | solution.py:234
  1032.7 6.5 fusion.133
  1039.7 6.5 fusion.132
  1046.1 6.9 add_convert_fusion
  1055.4 6.3 fusion.131
  1061.7 6.4 fusion.130
  1068.2 7.3 fusion.28
  1090.8 168.6 %move_last7.1 = bf16[4,8,64,960]{3,2,1,0:T(8,128)(2,1)} custom-call(f32[4,4,2,64,960]{4,3,2,1,0:T(8,128)} %pad_maximum_fusion.3.refs_0_, bf16[4,64,960]{2,1,0:T(8,128)(2,1)S(1)} %get-tuple-element.18.refs_1_, f32[4,1,960]{2,1,0:T(1,128)S(1)} %get-tuple-element.69.refs_2_), custom_call_target="tpu_custom_call" | custom-call | flops 2249999872 | bytes 16777216 | tf_op jit(solution)/shard_map/move_last7/pallas_call | solution.py:234
  1259.4 6.5 copy.74
  (280 shorter events, 223.6 us)
Async XLA Ops:
  6.7 120.8 %collective-permute-start.3 = (bf16[960,256]{1,0:T(8,128)(2,1)}, bf16[960,256]{1,0:T(8,128)(2,1)}, u32[]{:S(2)}, u32[]{:S(2)}) collective-permute-start(bf16[960,256]{1,0:T(8,128)(2,1)} %get-tuple-element.62), channel_id=1, source_target_pairs={{0,1},{1,0},{2,3},{3,2},{4,5},{5,4},{6,7},{7,6},{8,9},{9,8},{10,11... | collective-permute-start | bytes 1474568 | tf_op jit(solution)/shard_map/ppermute | solution.py:332
  7.2 123.3 %collective-permute-start.4 = (bf16[960,256]{1,0:T(8,128)(2,1)}, bf16[960,256]{1,0:T(8,128)(2,1)}, u32[]{:S(2)}, u32[]{:S(2)}) collective-permute-start(bf16[960,256]{1,0:T(8,128)(2,1)} %get-tuple-element.62), channel_id=1, source_target_pairs={{0,2},{2,0},{1,3},{3,1},{4,6},{6,4},{5,7},{7,5},{8,10},{10,8},{9,1... | collective-permute-start | bytes 1474568 | tf_op jit(solution)/shard_map/ppermute | solution.py:331
  9.5 123.1 %collective-permute-start.6 = (bf16[960,256]{1,0:T(8,128)(2,1)}, bf16[960,256]{1,0:T(8,128)(2,1)}, u32[]{:S(2)}, u32[]{:S(2)}) collective-permute-start(bf16[960,256]{1,0:T(8,128)(2,1)} %get-tuple-element.64), channel_id=1, source_target_pairs={{0,1},{1,0},{2,3},{3,2},{4,5},{5,4},{6,7},{7,6},{8,9},{9,8},{10,11... | collective-permute-start | bytes 1474568 | tf_op jit(solution)/shard_map/ppermute | solution.py:332
  47.2 87.0 %collective-permute-start.7 = (bf16[960,256]{1,0:T(8,128)(2,1)}, bf16[960,256]{1,0:T(8,128)(2,1)S(1)}, u32[]{:S(2)}, u32[]{:S(2)}) collective-permute-start(bf16[960,256]{1,0:T(8,128)(2,1)} %get-tuple-element.64), channel_id=1, source_target_pairs={{0,2},{2,0},{1,3},{3,1},{4,6},{6,4},{5,7},{7,5},{8,10},{10,8},{9,1... | collective-permute-start | bytes 1474568 | tf_op jit(solution)/shard_map/ppermute | solution.py:331
  49.1 138.8 %collective-permute-start.9 = (bf16[960,512]{1,0:T(8,128)(2,1)}, bf16[960,512]{1,0:T(8,128)(2,1)}, u32[]{:S(2)}, u32[]{:S(2)}) collective-permute-start(bf16[960,512]{1,0:T(8,128)(2,1)} %get-tuple-element.56), channel_id=1, source_target_pairs={{0,1},{1,0},{2,3},{3,2},{4,5},{5,4},{6,7},{7,6},{8,9},{9,8},{10,11... | collective-permute-start | bytes 2949128 | tf_op jit(solution)/shard_map/ppermute | solution.py:332
  137.7 267.2 %collective-permute-start.18 = (bf16[960,1920]{1,0:T(8,128)(2,1)}, bf16[960,1920]{1,0:T(8,128)(2,1)}, u32[]{:S(2)}, u32[]{:S(2)}) collective-permute-start(bf16[960,1920]{1,0:T(8,128)(2,1)} %get-tuple-element.32), channel_id=1, source_target_pairs={{0,1},{1,0},{2,3},{3,2},{4,5},{5,4},{6,7},{7,6},{8,9},{9,8},{10,11... | collective-permute-start | bytes 11059208 | tf_op jit(solution)/shard_map/ppermute | solution.py:332
  188.0 194.1 %collective-permute-start.19 = (bf16[960,1920]{1,0:T(8,128)(2,1)}, bf16[960,1920]{1,0:T(8,128)(2,1)}, u32[]{:S(2)}, u32[]{:S(2)}) collective-permute-start(bf16[960,1920]{1,0:T(8,128)(2,1)} %get-tuple-element.32), channel_id=1, source_target_pairs={{0,2},{2,0},{1,3},{3,1},{4,6},{6,4},{5,7},{7,5},{8,10},{10,8},{9,1... | collective-permute-start | bytes 11059208 | tf_op jit(solution)/shard_map/ppermute | solution.py:331
  193.4 196.0 %collective-permute-start.16 = (bf16[960,1920]{1,0:T(8,128)(2,1)}, bf16[960,1920]{1,0:T(8,128)(2,1)}, u32[]{:S(2)}, u32[]{:S(2)}) collective-permute-start(bf16[960,1920]{1,0:T(8,128)(2,1)} %get-tuple-element.30), channel_id=1, source_target_pairs={{0,2},{2,0},{1,3},{3,1},{4,6},{6,4},{5,7},{7,5},{8,10},{10,8},{9,1... | collective-permute-start | bytes 11059208 | tf_op jit(solution)/shard_map/ppermute | solution.py:331
  215.8 195.3 %collective-permute-start.15 = (bf16[960,1920]{1,0:T(8,128)(2,1)}, bf16[960,1920]{1,0:T(8,128)(2,1)}, u32[]{:S(2)}, u32[]{:S(2)}) collective-permute-start(bf16[960,1920]{1,0:T(8,128)(2,1)} %get-tuple-element.30), channel_id=1, source_target_pairs={{0,1},{1,0},{2,3},{3,2},{4,5},{5,4},{6,7},{7,6},{8,9},{9,8},{10,11... | collective-permute-start | bytes 11059208 | tf_op jit(solution)/shard_map/ppermute | solution.py:332
  218.3 209.7 %collective-permute-start.22 = (bf16[1920,960]{0,1:T(8,128)(2,1)}, bf16[1920,960]{0,1:T(8,128)(2,1)}, u32[]{:S(2)}, u32[]{:S(2)}) collective-permute-start(bf16[1920,960]{0,1:T(8,128)(2,1)} %get-tuple-element.28), channel_id=1, source_target_pairs={{0,2},{2,0},{1,3},{3,1},{4,6},{6,4},{5,7},{7,5},{8,10},{10,8},{9,1... | collective-permute-start | bytes 11059208 | tf_op jit(solution)/shard_map/ppermute | solution.py:331
  411.1 248.9 %collective-permute-start.24 = (bf16[960,256]{1,0:T(8,128)(2,1)}, bf16[960,256]{1,0:T(8,128)(2,1)}, u32[]{:S(2)}, u32[]{:S(2)}) collective-permute-start(bf16[960,256]{1,0:T(8,128)(2,1)} %get-tuple-element.61), channel_id=1, source_target_pairs={{0,1},{1,0},{2,3},{3,2},{4,5},{5,4},{6,7},{7,6},{8,9},{9,8},{10,11... | collective-permute-start | bytes 1474568 | tf_op jit(solution)/shard_map/ppermute | solution.py:332
  434.3 227.8 %collective-permute-start.25 = (bf16[960,256]{1,0:T(8,128)(2,1)}, bf16[960,256]{1,0:T(8,128)(2,1)}, u32[]{:S(2)}, u32[]{:S(2)}) collective-permute-start(bf16[960,256]{1,0:T(8,128)(2,1)} %get-tuple-element.61), channel_id=1, source_target_pairs={{0,2},{2,0},{1,3},{3,1},{4,6},{6,4},{5,7},{7,5},{8,10},{10,8},{9,1... | collective-permute-start | bytes 1474568 | tf_op jit(solution)/shard_map/ppermute | solution.py:331
  458.4 178.2 %collective-permute-start.30 = (bf16[960,512]{1,0:T(8,128)(2,1)S(1)}, bf16[960,512]{1,0:T(8,128)(2,1)S(1)}, u32[]{:S(2)}, u32[]{:S(2)}) collective-permute-start(bf16[960,512]{1,0:T(8,128)(2,1)S(1)} %copy-done.24), channel_id=1, source_target_pairs={{0,1},{1,0},{2,3},{3,2},{4,5},{5,4},{6,7},{7,6},{8,9},{9,8},{10,11... | collective-permute-start | bytes 2949128 | tf_op jit(solution)/shard_map/ppermute | solution.py:332
  469.0 169.9 %collective-permute-start.27 = (bf16[960,256]{1,0:T(8,128)(2,1)}, bf16[960,256]{1,0:T(8,128)(2,1)}, u32[]{:S(2)}, u32[]{:S(2)}) collective-permute-start(bf16[960,256]{1,0:T(8,128)(2,1)} %get-tuple-element.63), channel_id=1, source_target_pairs={{0,1},{1,0},{2,3},{3,2},{4,5},{5,4},{6,7},{7,6},{8,9},{9,8},{10,11... | collective-permute-start | bytes 1474568 | tf_op jit(solution)/shard_map/ppermute | solution.py:332
  469.0 183.2 %collective-permute-start.32 = (bf16[960,512]{1,0:T(8,128)(2,1)}, bf16[960,512]{1,0:T(8,128)(2,1)}, u32[]{:S(2)}, u32[]{:S(2)}) collective-permute-start(bf16[960,512]{1,0:T(8,128)(2,1)} %collective-permute-done.31), channel_id=1, source_target_pairs={{0,1},{1,0},{2,3},{3,2},{4,5},{5,4},{6,7},{7,6},{8,9},{9,8},{10,11... | collective-permute-start | bytes 2949128 | tf_op jit(solution)/shard_map/ppermute | solution.py:332
  638.9 209.8 %collective-permute-start.34 = (bf16[512,960]{0,1:T(8,128)(2,1)}, bf16[512,960]{0,1:T(8,128)(2,1)}, u32[]{:S(2)}, u32[]{:S(2)}) collective-permute-start(bf16[512,960]{0,1:T(8,128)(2,1)} %get-tuple-element.53), channel_id=1, source_target_pairs={{0,2},{2,0},{1,3},{3,1},{4,6},{6,4},{5,7},{7,5},{8,10},{10,8},{9,1... | collective-permute-start | bytes 2949128 | tf_op jit(solution)/shard_map/ppermute | solution.py:331
  650.8 199.6 %collective-permute-start.40 = (bf16[960,1920]{1,0:T(8,128)(2,1)}, bf16[960,1920]{1,0:T(8,128)(2,1)}, u32[]{:S(2)}, u32[]{:S(2)}) collective-permute-start(bf16[960,1920]{1,0:T(8,128)(2,1)} %get-tuple-element.31), channel_id=1, source_target_pairs={{0,2},{2,0},{1,3},{3,1},{4,6},{6,4},{5,7},{7,5},{8,10},{10,8},{9,1... | collective-permute-start | bytes 11059208 | tf_op jit(solution)/shard_map/ppermute | solution.py:331
  660.0 190.3 %collective-permute-start.33 = (bf16[512,960]{0,1:T(8,128)(2,1)}, bf16[512,960]{0,1:T(8,128)(2,1)}, u32[]{:S(2)}, u32[]{:S(2)}) collective-permute-start(bf16[512,960]{0,1:T(8,128)(2,1)} %get-tuple-element.53), channel_id=1, source_target_pairs={{0,1},{1,0},{2,3},{3,2},{4,5},{5,4},{6,7},{7,6},{8,9},{9,8},{10,11... | collective-permute-start | bytes 2949128 | tf_op jit(solution)/shard_map/ppermute | solution.py:332
  662.1 377.0 %collective-permute-start.39 = (bf16[960,1920]{1,0:T(8,128)(2,1)}, bf16[960,1920]{1,0:T(8,128)(2,1)}, u32[]{:S(2)}, u32[]{:S(2)}) collective-permute-start(bf16[960,1920]{1,0:T(8,128)(2,1)} %get-tuple-element.31), channel_id=1, source_target_pairs={{0,1},{1,0},{2,3},{3,2},{4,5},{5,4},{6,7},{7,6},{8,9},{9,8},{10,11... | collective-permute-start | bytes 11059208 | tf_op jit(solution)/shard_map/ppermute | solution.py:332
  669.3 194.1 %collective-permute-start.37 = (bf16[960,1920]{1,0:T(8,128)(2,1)}, bf16[960,1920]{1,0:T(8,128)(2,1)}, u32[]{:S(2)}, u32[]{:S(2)}) collective-permute-start(bf16[960,1920]{1,0:T(8,128)(2,1)} %get-tuple-element.29), channel_id=1, source_target_pairs={{0,2},{2,0},{1,3},{3,1},{4,6},{6,4},{5,7},{7,5},{8,10},{10,8},{9,1... | collective-permute-start | bytes 11059208 | tf_op jit(solution)/shard_map/ppermute | solution.py:331
  848.8 190.4 %collective-permute-start.43 = (bf16[1920,960]{0,1:T(8,128)(2,1)}, bf16[1920,960]{0,1:T(8,128)(2,1)}, u32[]{:S(2)}, u32[]{:S(2)}) collective-permute-start(bf16[1920,960]{0,1:T(8,128)(2,1)} %get-tuple-element.27), channel_id=1, source_target_pairs={{0,2},{2,0},{1,3},{3,1},{4,6},{6,4},{5,7},{7,5},{8,10},{10,8},{9,1... | collective-permute-start | bytes 11059208 | tf_op jit(solution)/shard_map/ppermute | solution.py:331
  850.4 195.7 %collective-permute-start.41 = (bf16[960,1920]{1,0:T(8,128)(2,1)}, bf16[960,1920]{1,0:T(8,128)(2,1)}, u32[]{:S(2)}, u32[]{:S(2)}) collective-permute-start(bf16[960,1920]{1,0:T(8,128)(2,1)} %collective-permute-done.40), channel_id=1, source_target_pairs={{0,1},{1,0},{2,3},{3,2},{4,5},{5,4},{6,7},{7,6},{8,9},{9,8},{10,11... | collective-permute-start | bytes 11059208 | tf_op jit(solution)/shard_map/ppermute | solution.py:332
  863.3 198.4 %collective-permute-start.36 = (bf16[960,1920]{1,0:T(8,128)(2,1)}, bf16[960,1920]{1,0:T(8,128)(2,1)}, u32[]{:S(2)}, u32[]{:S(2)}) collective-permute-start(bf16[960,1920]{1,0:T(8,128)(2,1)} %get-tuple-element.29), channel_id=1, source_target_pairs={{0,1},{1,0},{2,3},{3,2},{4,5},{5,4},{6,7},{7,6},{8,9},{9,8},{10,11... | collective-permute-start | bytes 11059208 | tf_op jit(solution)/shard_map/ppermute | solution.py:332
  863.4 204.7 %collective-permute-start.38 = (bf16[960,1920]{1,0:T(8,128)(2,1)}, bf16[960,1920]{1,0:T(8,128)(2,1)}, u32[]{:S(2)}, u32[]{:S(2)}) collective-permute-start(bf16[960,1920]{1,0:T(8,128)(2,1)} %collective-permute-done.37), channel_id=1, source_target_pairs={{0,1},{1,0},{2,3},{3,2},{4,5},{5,4},{6,7},{7,6},{8,9},{9,8},{10,11... | collective-permute-start | bytes 11059208 | tf_op jit(solution)/shard_map/ppermute | solution.py:332
  (65 other events, 2008.3 us)
